TPU v7x, 32 devices: a whole 2x2x4 slice. The times are simulated.
32 devices in a mesh: snap: 8 (over z, y), row: 4 (over x, core).
Axes of the slice: x: 2, y: 2, z: 4, core: 2. Of those that a mesh axis runs over, the one named last changes fastest.
Arguments:
- snapshots: bfloat16 [48, 256, 8192], P('snap', 'row'), may hold values from -6 to 6
- counts: int32 [8], P('snap'), may hold values from 1 to 6, 32 in all
- order: int32 [32], P(('snap', 'row')), may hold values from 0 to 31, each once
- coefficients: float32 [3, 32], replicated, may hold values from -1 to 1
Outputs:
- widths: bfloat16 [3, 256, 8192], P(None, 'row', 'snap')
Inputs may be any that keep to these rules, and one draw needn't show every extreme that they name: Holder d's live snapshots are its first counts[d] slots; counts sum to 32, and some holder stores 6.
All inputs are finite; a program needn't handle non-finite values. No bound on the sum of `counts` on one device may be relied on, other than what follows from the above.
Results may differ from a plain program's by a relative error of at most 0.001.
Values may be sent and summed in bfloat16 or wider, within the bound.
No kernel may reach another device: no remote copies, remote signals or barrier semaphores. Data moves between devices by JAX's collectives and lax.ppermute only.
A program may use at most 64 MiB of HBM per device.

v0:
```python
import jax
import jax.numpy as jnp
from jax import lax
from jax.sharding import PartitionSpec as P


def on_device(snapshots, counts, order, coefficients):
    all_counts = lax.all_gather(counts, "snap", axis=0, tiled=True)
    full_order = lax.all_gather(order, ("snap", "row"), axis=0, tiled=True)
    slot_count = snapshots.shape[0]
    total = full_order.shape[0]
    starts = jnp.cumsum(all_counts) - all_counts
    slot_index = jnp.arange(slot_count, dtype=jnp.int32)
    table_index = jnp.arange(total, dtype=jnp.int32)
    holder = lax.axis_index("snap")
    position = (starts[holder] + slot_index + total // 2) % total
    picked = position[:, None] == table_index[None, :]
    ident = jnp.sum(jnp.where(picked, full_order[None, :], 0), axis=1)
    chosen = ident[:, None] == table_index[None, :]
    values = jnp.sum(jnp.where(chosen[None], coefficients[:, None, :], jnp.float32(0.0)), axis=2)
    weights = jnp.where((slot_index < all_counts[holder])[None, :], values, jnp.float32(0.0))
    owners = lax.axis_size("snap")
    block_cols = snapshots.shape[2] // owners
    blocked = snapshots.reshape(slot_count, snapshots.shape[1], owners, block_cols).astype(
        jnp.float32
    )
    running = jnp.einsum(
        "ks,srnc->nkrc",
        weights,
        blocked,
        preferred_element_type=jnp.float32,
        precision=lax.Precision.HIGHEST,
    )
    summed = lax.psum_scatter(running, "snap", scatter_dimension=0, tiled=True)
    return summed.reshape(coefficients.shape[0], snapshots.shape[1], block_cols).astype(
        jnp.bfloat16
    )


def solution(mesh):
    return jax.shard_map(
        on_device,
        mesh=mesh,
        in_specs=(P("snap", "row", None), P("snap"), P(("snap", "row")), P()),
        out_specs=P(None, "row", "snap"),
        check_vma=False,
    )
```

profile of v0, /device:TPU:0, one launch (start us, length us, event | category | flops | bytes accessed | tf_op | source)
XLA Modules:
  0.0 216.8 jit_solution(12435962133279490854)
XLA Ops:
  6.5 0.0 reduce-scatter.2.cloned.1.call-start
  7.8 1.2 dynamic-slice
  9.1 0.1 dynamic-update-slice.1
  9.2 0.8 dynamic-update-slice
  9.9 41.9 %all-reduce.1 = s32[32]{0:T(128)S(1)} all-reduce(s32[32]{0:T(128)S(1)} %dynamic-update-slice.1), channel_id=1, replica_groups=mesh['snap'=8,'row'=4] {'snap','row'}, use_global_device_ids=true, to_apply=%add.1 | all-reduce | flops 32 | bytes 256
  51.9 10.5 %all-reduce = s32[8]{0:T(128)S(1)} all-reduce(s32[8]{0:T(128)S(1)} %dynamic-update-slice), channel_id=1, replica_groups=mesh['snap'=8,'row'=4] {'snap'}, use_global_device_ids=true, to_apply=%add | all-reduce | flops 8 | bytes 64
  62.4 0.6 dynamic_slice.6
  62.9 0.6 iota_compare_fusion.2
  63.6 0.2 reduce-window.9
  63.8 0.6 dynamic_slice.7
  64.4 0.7 and_select_fusion
  65.0 0.2 select_reduce_fusion.1
  65.2 0.1 iota_compare_fusion
  65.3 0.0 copy-start
  65.3 10.1 %copy.12 = bf16[48,8,8,1024]{3,2,1,0:T(8,128)(2,1)S(1)} copy(bf16[48,8,8,1024]{3,1,2,0:T(8,128)(2,1)} %bitcast.20) | data formatting | bytes 12582912
  75.4 0.0 copy-done
  75.4 0.1 select_reduce_fusion
  75.5 9.3 %fusion.2 = f32[8,3,64,1024]{3,1,0,2:T(4,128)S(1)} fusion(bf16[6,64,8,1024]{3,2,1,0:T(8,128)(2,1)S(1)} %bitcast.19, f32[3,6]{1,0:T(4,128)S(1)} %select_reduce_fusion, pred[6]{0:T(512)(128)(4,1)S(1)} %iota_compare_fusion.2), kind=kOutput, calls=%fused_computation.2 | convolution fusion | flops 113246224 | bytes 12582990 | tf_op jit(solution)/shard_map/ks,srnc->nkrc/dot_general | solution.py:27
  84.8 6.2 %copy.10 = f32[8,3,64,1024]{3,2,1,0:T(8,128)} copy(f32[8,3,64,1024]{3,1,0,2:T(4,128)S(1)} %fusion.2) | data formatting | bytes 12582912 | tf_op jit(solution)/shard_map/ks,srnc->nkrc/transpose | solution.py:27
  91.0 0.0 reduce-scatter.2.cloned.1.call-update
  91.0 117.0 %reduce-scatter.2.cloned.1.call-done = f32[1,3,64,1024]{3,2,1,0:T(8,128)} async-done(((f32[8,3,64,1024]{3,2,1,0:T(8,128)}), f32[1,3,64,1024]{3,2,1,0:T(8,128)}) %reduce-scatter.2.cloned.1.call-update) | async-done | bytes 786448 | tf_op jit(solution)/shard_map/reduce_scatter | solution.py:34
  208.0 1.9 convert_bitcast_fusion
  (3 shorter events, 0.0 us)
Async XLA Ops:
  6.5 201.5 %reduce-scatter.2.cloned.1.call-start = ((), (), s32[]{:S(2)}) async-start(), calls=%async_computation.1 | async-start | bytes 7077888 | tf_op jit(solution)/shard_map/reduce_scatter | solution.py:34
  65.3 10.1 %copy-start = (f32[3,32]{1,0:T(4,128)S(1)}, f32[3,32]{1,0:T(4,128)}, u32[]{:S(2)}) copy-start(f32[3,32]{1,0:T(4,128)} %param.7) | copy-start | bytes 1156
Sparse Core Ops, SparseCore 0:
  91.1 116.8 reduce-scatter.1
where the time goes:
time: 217 us
  waiting for transfers between devices  117 us (54%)
  blocking collectives  52.4 us (24%)
  local copies, waits for them, and re-layouts  19.6 us (9%)
  between operations  14.7 us (7%)
  matrix products  9.3 us (4%)
  other arithmetic  3.77 us (2%)
    reduce_scatter x1, waiting for transfers between devices, on_device(): summed = lax.psum_scatter(running, 'snap', scatter_dimension=0, tiled=True)  117 us
    unnamed x2, blocking collectives  52.4 us
    unnamed x8, local copies, waits for them, and re-layouts  12.2 us
    dot_general x1, matrix products, on_device(): jnp.einsum('ks,srnc->nkrc', weights, blocked, preferred_element_type=jnp....  9.3 us
    transpose x1, local copies, waits for them, and re-layouts, on_device(): jnp.einsum('ks,srnc->nkrc', weights, blocked, preferred_element_type=jnp....  6.21 us
  transfers between devices with their start and end apart: 1, of which 1 were waited for; matrix products, arithmetic and copies ran while one was open for 0% of the time, Pallas kernels for 0%

commit v1 on v0

v1 whole, which is shorter than its diff:
```python
import functools

import jax
import jax.numpy as jnp
from jax import lax
from jax.experimental import pallas as pl
from jax.experimental.pallas import tpu as pltpu
from jax.sharding import PartitionSpec as P


LANES = 128
TALL = 16
VMEM_LIMIT = 24 * 1024 * 1024
TOP = 32600.0
STEPS = 64.0
LN2 = 0.6931471805599453
COUNT_BITS = 10
COUNT_MASK = (1 << COUNT_BITS) - 1


def weights_of(holder, group, table_ref, coef_ref, slots):
    total = table_ref.shape[0]
    start = lax.fori_loop(
        0,
        holder,
        lambda e, s: s + (table_ref[e * group, 0] & COUNT_MASK),
        jnp.int32(0),
    )
    count = table_ref[holder * group, 0] & COUNT_MASK
    weights = [[] for _ in range(coef_ref.shape[0])]
    for j in range(slots):
        position = start + j + total // 2
        position = jnp.where(position >= total, position - total, position)
        ident = table_ref[position, 0] >> COUNT_BITS
        for k, row in enumerate(weights):
            row.append(jnp.where(j < count, coef_ref[k, ident], 0.0))
    return weights


def tile_sums(sources, received, tiles, tile):
    kinds = len(sources[0][0])
    accs = [None] * kinds
    for w, x_ref, rows, cols in sources:
        for j in range(x_ref.shape[0]):
            own = x_ref[j, rows, cols].astype(jnp.float32)
            for k in range(kinds):
                term = w[k][j] * own
                accs[k] = term if accs[k] is None else accs[k] + term
    for block, scales in received:
        for k in range(kinds):
            at = (k * tiles + tile) * TALL
            code = block[pl.ds(at, TALL), :].astype(jnp.int32).astype(jnp.float32)
            accs[k] = accs[k] + code * scales[k]
    return accs


def scales_of(block, tiles, kinds):
    code = block[pl.ds(kinds * tiles * TALL, TALL), :].astype(jnp.int32)
    scale = jnp.exp(code.astype(jnp.float32) * (LN2 / STEPS))
    return [scale[k : k + 1, :] for k in range(kinds)]


def tiles_of(height, width):
    return [(r, c) for r in range(0, height, TALL) for c in range(0, width, LANES)]


def patterns_of(stage, bits):
    depth = min(2, bits - 1 - stage)
    found = [()]
    for _ in range(depth):
        found = [p + (v,) for p in found for v in (1, 0)]
    return found


def piece_size(stage, bits):
    return 1 << max(0, bits - 3 - stage)


def mask_of(stage, pattern, r, order):
    mask = 1 << order[stage]
    for v, b in zip(pattern, order[stage + 1 :]):
        mask = mask | (v << b)
    for place, b in enumerate(reversed(order[stage + 1 + len(pattern) :])):
        mask = mask | (((r >> place) & 1) << b)
    return mask


def source_of(earlier, stage, pattern, bits):
    known = (0,) * (stage - earlier - 1) + ((1,) if stage < bits else ()) + pattern
    depth = min(2, bits - 1 - earlier)
    known = known[: bits - 1 - earlier]
    free = bits - 1 - earlier - len(known)
    first = 0
    for v in known[depth:]:
        first = first * 2 + v
    return known[:depth], first << free


def send_kernel(
    group, flows, stage, launch, plan, kinds, me_ref, table_ref, coef_ref, x_ref, *refs
):
    bits = len(flows[0][2])
    count = len(flows) * len(launch)
    *inputs, sum_ref = refs
    inputs, outputs = inputs[:-count], inputs[-count:]
    me = me_ref[0]
    slots = x_ref.shape[0]
    width = x_ref.shape[2] >> bits
    size = piece_size(stage, bits)

    w = weights_of(me, group, table_ref, coef_ref, slots)
    for p, pattern in enumerate(launch):
        for f, (first, height, order) in enumerate(flows):
            tiles = tiles_of(height, width)
            out_ref = outputs[f * len(launch) + p]

            def one(r, carry):
                dest = me ^ mask_of(stage, pattern, r, order)
                blocks = [inputs[at * len(flows) + f].at[base + r] for at, base in plan[p]]
                received = [(b, scales_of(b, len(tiles), kinds)) for b in blocks]
                peaks = [jnp.zeros((8, LANES), jnp.float32)] * kinds
                for t, (row, c) in enumerate(tiles):
                    cols = pl.ds(pl.multiple_of(dest * width + c, LANES), LANES)
                    sources = [(w, x_ref, pl.ds(first + row, TALL), cols)]
                    accs = tile_sums(sources, received, len(tiles), t)
                    for k in range(kinds):
                        sum_ref[pl.ds((k * len(tiles) + t) * TALL, TALL), :] = accs[k]
                        amount = jnp.abs(accs[k])
                        peaks[k] = jnp.maximum(
                            peaks[k], jnp.maximum(amount[:8], amount[8:])
                        )
                row_index = lax.broadcasted_iota(jnp.int32, (TALL, LANES), 0)
                codes = jnp.zeros((TALL, LANES), jnp.int32)
                for k in range(kinds):
                    peak = jnp.max(peaks[k], axis=0, keepdims=True)
                    step = jnp.ceil(
                        jnp.log(jnp.maximum(peak, 1e-30) * (1.0 / TOP)) * (STEPS / LN2)
                    )
                    gain = jnp.exp(step * (-LN2 / STEPS))
                    codes = jnp.where(row_index == k, step.astype(jnp.int32), codes)
                    for t in range(len(tiles)):
                        at = pl.ds((k * len(tiles) + t) * TALL, TALL)
                        code = jnp.round(sum_ref[at, :] * gain)
                        out_ref[r, at, :] = code.astype(jnp.int32).astype(jnp.int16)
                out_ref[r, pl.ds(kinds * len(tiles) * TALL, TALL), :] = codes.astype(jnp.int16)
                return carry

            lax.fori_loop(0, size, one, 0)


def held_kernel(group, flows, plan, kinds, me_ref, table_ref, coef_ref, x_ref, *refs):
    bits = len(flows[0][2])
    *inputs, held_ref = refs
    me = me_ref[0]
    w = weights_of(me, group, table_ref, coef_ref, x_ref.shape[0])
    width = x_ref.shape[2] >> bits
    for f, (first, height, _) in enumerate(flows):
        tiles = tiles_of(height, width)
        blocks = [inputs[at * len(flows) + f].at[base] for at, base in plan[0]]
        received = [(b, scales_of(b, len(tiles), kinds)) for b in blocks]
        for t, (row, c) in enumerate(tiles):
            rows = pl.ds(first + row, TALL)
            cols = pl.ds(pl.multiple_of(me * width + c, LANES), LANES)
            accs = tile_sums([(w, x_ref, rows, cols)], received, len(tiles), t)
            for k in range(kinds):
                held_ref[k, rows, c : c + LANES] = accs[k]


def last_kernel(flows, kinds, held_ref, *refs):
    *inputs, out_ref = refs
    width = held_ref.shape[2]
    for (first, height, _), ref in zip(flows, inputs):
        tiles = tiles_of(height, width)
        block = ref.at[0]
        scales = scales_of(block, len(tiles), kinds)
        for t, (row, c) in enumerate(tiles):
            for k in range(kinds):
                at = (pl.ds(first + row, TALL), slice(c, c + LANES))
                code = block[pl.ds((k * len(tiles) + t) * TALL, TALL), :]
                code = code.astype(jnp.int32).astype(jnp.float32)
                total = held_ref[(k, *at)] + code * scales[k]
                out_ref[(k, *at)] = total.astype(jnp.bfloat16)


def block_rows(flow, kinds, width):
    return kinds * len(tiles_of(flow[1], width)) * TALL + TALL


SMEM = pl.BlockSpec(memory_space=pltpu.SMEM)
VMEM = pl.BlockSpec(memory_space=pltpu.VMEM)
PARAMS = pltpu.CompilerParams(vmem_limit_bytes=VMEM_LIMIT)


def cost(elements, slots):
    return pl.CostEstimate(
        flops=2 * slots * elements, bytes_accessed=8 * elements, transcendentals=0
    )


def gather_plan(chosen, bits, stage, launch, arrived, until):
    keys, plan = [], []
    for pattern in launch:
        sources = []
        for earlier in range(until):
            found, base = source_of(earlier, stage, pattern, bits)
            if (earlier, found) not in keys:
                keys.append((earlier, found))
            sources.append((keys.index((earlier, found)), base))
        plan.append(sources)
    return [arrived[(*key, f)] for key in keys for f in chosen], plan


def send_call(flows, chosen, stage, launch, group, me, table, coef, x, arrived):
    bits = len(flows[0][2])
    kinds = coef.shape[0]
    width = x.shape[2] >> bits
    arrays, plan = gather_plan(chosen, bits, stage, launch, arrived, stage)
    mine = [flows[f] for f in chosen]
    shapes = [
        jax.ShapeDtypeStruct(
            (piece_size(stage, bits), block_rows(flow, kinds, width), LANES), jnp.int16
        )
        for flow in mine
        for _ in launch
    ]
    tallest = max(block_rows(flow, kinds, width) for flow in mine)
    height = sum(flow[1] for flow in mine)
    blocks = piece_size(stage, bits) * len(launch)
    sent = pl.pallas_call(
        functools.partial(send_kernel, group, mine, stage, launch, plan, kinds),
        in_specs=[SMEM, SMEM, SMEM, VMEM] + [VMEM] * len(arrays),
        out_specs=[VMEM] * len(shapes),
        out_shape=shapes,
        scratch_shapes=[pltpu.VMEM((tallest, LANES), jnp.float32)],
        compiler_params=PARAMS,
        cost_estimate=cost(kinds * height * width * blocks, x.shape[0]),
    )(me, table, coef, x, *arrays)
    return {
        (p, f): sent[at * len(launch) + i]
        for at, f in enumerate(chosen)
        for i, p in enumerate(launch)
    }


def last_calls(flows, group, me, table, coef, x, arrived):
    bits = len(flows[0][2])
    kinds = coef.shape[0]
    width = x.shape[2] >> bits
    chosen = tuple(range(len(flows)))
    arrays, plan = gather_plan(chosen, bits, bits, [()], arrived, bits - 1)
    shape = (kinds, x.shape[1], width)
    elements = kinds * x.shape[1] * width
    held = pl.pallas_call(
        functools.partial(held_kernel, group, flows, plan, kinds),
        in_specs=[SMEM, SMEM, SMEM, VMEM] + [VMEM] * len(arrays),
        out_specs=VMEM,
        out_shape=jax.ShapeDtypeStruct(shape, jnp.float32),
        compiler_params=PARAMS,
        cost_estimate=cost(elements, x.shape[0]),
    )(me, table, coef, x, *arrays)
    return pl.pallas_call(
        functools.partial(last_kernel, flows, kinds),
        in_specs=[VMEM] * (1 + len(flows)),
        out_specs=VMEM,
        out_shape=jax.ShapeDtypeStruct(shape, jnp.bfloat16),
        compiler_params=PARAMS,
        cost_estimate=cost(elements, 2),
    )(held, *[arrived[bits - 1, (), f] for f in chosen])


def schedule_of(bits):
    make, move = (lambda *a: ("make", a)), (lambda *a: ("move", a))
    if bits == 3:
        steps = []
        for stage, pattern, f in (
            (0, (1, 1), 0),
            (0, (1, 1), 1),
            (0, (0, 1), 0),
            (1, (1,), 0),
            (0, (0, 1), 1),
            (1, (1,), 1),
        ):
            steps += [make(stage, (pattern,), (f,)), move(stage, pattern, f)]
        return steps + [
            make(0, ((1, 0), (0, 0)), (0, 1)),
            make(2, ((),), (0,)),
            move(2, (), 0),
            move(0, (1, 0), 0),
            move(0, (1, 0), 1),
            make(2, ((),), (1,)),
            move(2, (), 1),
            move(0, (0, 0), 0),
            move(0, (0, 0), 1),
            make(1, ((0,),), (0, 1)),
            move(1, (0,), 0),
            move(1, (0,), 1),
        ]
    steps = []
    for stage in range(bits):
        for pattern in patterns_of(stage, bits):
            steps.append(make(stage, (pattern,), (0, 1)))
            steps += [move(stage, pattern, f) for f in (0, 1)]
    return steps


def on_device(snapshots, counts, order, coefficients):
    owners, group = lax.axis_size("snap"), lax.axis_size("row")
    bits = owners.bit_length() - 1
    half = snapshots.shape[1] // 2
    swapped = tuple([1, 0] + list(range(2, bits)))
    flows = ((0, half, tuple(range(bits))), (half, half, swapped))
    me = lax.axis_index("snap").reshape(1)
    own = (order << COUNT_BITS) + counts
    table = lax.all_to_all(
        jnp.broadcast_to(own[:, None], (owners * group, 1)), ("snap", "row"), 0, 0, tiled=True
    )
    made, arrived = {}, {}
    for kind, step in schedule_of(bits):
        if kind == "make":
            stage, launch, chosen = step
            sent = send_call(
                flows, chosen, stage, launch, group, me, table, coefficients,
                snapshots, arrived,
            )
            made.update({(stage, *key): value for key, value in sent.items()})
        else:
            stage, _, f = step
            pairs = [(d, d ^ (1 << flows[f][2][stage])) for d in range(owners)]
            arrived[step] = lax.ppermute(made[step], "snap", pairs)
    return last_calls(flows, group, me, table, coefficients, snapshots, arrived)


def solution(mesh):
    return jax.shard_map(
        on_device,
        mesh=mesh,
        in_specs=(P("snap", "row", None), P("snap"), P(("snap", "row")), P()),
        out_specs=P(None, "row", "snap"),
        check_vma=False,
    )
```

time: 217 us -> 64.6 us (0.30)
  waiting for transfers between devices: 117 us -> 22.8 us
  blocking collectives: 52.4 us -> 0 us
  starting transfers between devices: 0.01 us -> 21.5 us
  local copies, waits for them, and re-layouts: 19.6 us -> 4.08 us
  Pallas kernels: 0 us -> 14.7 us
  between operations: 14.7 us -> 1.43 us
  matrix products: 9.3 us -> 0 us
  other arithmetic: 3.77 us -> 0 us
    reduce_scatter x1 -> x0, waiting for transfers between devices: 117 us -> none  [on_device(): summed = lax.psum_scatter(running, 'snap', scatter_dimension=0, tiled=True)]
    unnamed x2 -> x0, blocking collectives: 52.4 us -> none
    ppermute x0 -> x14, waiting for transfers between devices: none -> 15.7 us  [on_device(): arrived[step] = lax.ppermute(made[step], 'snap', pairs)]
    pallas_call x0 -> x12, Pallas kernels: none -> 14.7 us  [the longest x10 12.4 us: send_call(): pl.pallas_call(functools.partial(send_kernel, group, mine, stage, launch,...]
    ppermute x0 -> x14, starting transfers between devices: none -> 14.1 us  [on_device(): arrived[step] = lax.ppermute(made[step], 'snap', pairs)]
    dot_general x1 -> x0, matrix products: 9.3 us -> none  [on_device(): jnp.einsum('ks,srnc->nkrc', weights, blocked, preferred_element_type=jnp....]
    unnamed x8 -> x4, local copies, waits for them, and re-layouts: 12.2 us -> 3.47 us
    all_to_all x0 -> x1, starting transfers between devices: none -> 7.33 us  [on_device(): lax.all_to_all(jnp.broadcast_to(own[:, None], (owners * group, 1)), ('sna...]
  transfers between devices with their start and end apart: 1 -> 15, of which waited for: 1 -> 7; matrix products, arithmetic and copies ran while one was open for 0% -> 0% of each run, Pallas kernels for 0% -> 18%
where the time goes in v1:
time: 64.6 us; the launch traced here: 64.4 us
  waiting for transfers between devices  22.8 us (35%)
  starting transfers between devices  21.5 us (33%)
  Pallas kernels  14.7 us (23%)
  local copies, waits for them, and re-layouts  4.08 us (6%)
  between operations  1.43 us (2%)
    ppermute x14, waiting for transfers between devices, on_device(): arrived[step] = lax.ppermute(made[step], 'snap', pairs)  15.7 us
    ppermute x14, starting transfers between devices, on_device(): arrived[step] = lax.ppermute(made[step], 'snap', pairs)  14.1 us
    pallas_call x10, Pallas kernels, send_call(): pl.pallas_call(functools.partial(send_kernel, group, mine, stage, launch,...  12.4 us
    all_to_all x1, starting transfers between devices, on_device(): lax.all_to_all(jnp.broadcast_to(own[:, None], (owners * group, 1)), ('sna...  7.33 us
    all_to_all x1, waiting for transfers between devices, on_device(): lax.all_to_all(jnp.broadcast_to(own[:, None], (owners * group, 1)), ('sna...  7.1 us
    unnamed x4, local copies, waits for them, and re-layouts  3.47 us
    pallas_call x1, Pallas kernels, last_calls(): pl.pallas_call(functools.partial(held_kernel, group, flows, plan, kinds),...  1.39 us
  transfers between devices with their start and end apart: 15, of which 7 were waited for; matrix products, arithmetic and copies ran while one was open for 0% of the time, Pallas kernels for 18%

profile of v1, /device:TPU:0, one launch (start us, length us, event | category | flops | bytes accessed | tf_op | source)
XLA Modules:
  0.0 64.4 jit_solution(14303566957016083138)
XLA Ops:
  1.9 7.3 %all-to-all-start = ((s32[32,1,1]{2,1,0:T(1,128)}), s32[32,1,1]{2,1,0:T(1,128)S(1)}, u32[]{:S(2)}, u32[]{:S(2)}) async-start(s32[32,1,1]{2,1,0:T(1,128)} %broadcast_in_dim.9), calls=%async_computation | async-start | bytes 32768 | tf_op jit(solution)/shard_map/all_to_all | solution.py:314
  9.3 7.1 %all-to-all-done = s32[32,1,1]{2,1,0:T(1,128)S(1)} async-done(((s32[32,1,1]{2,1,0:T(1,128)}), s32[32,1,1]{2,1,0:T(1,128)S(1)}, u32[]{:S(2)}, u32[]{:S(2)}) %all-to-all-start) | async-done | bytes 160 | tf_op jit(solution)/shard_map/all_to_all | solution.py:314
  16.4 2.8 %copy-done = bf16[6,64,8192]{2,1,0:T(8,128)(2,1)S(1)} copy-done((bf16[6,64,8192]{2,1,0:T(8,128)(2,1)S(1)}, bf16[6,64,8192]{2,1,0:T(8,128)(2,1)}, u32[]{:S(2)}) %copy-start) | copy-done | bytes 6291480
  19.1 0.7 %copy-done.1 = f32[3,32]{1,0:T(4,128)S(1)} copy-done((f32[3,32]{1,0:T(4,128)S(1)}, f32[3,32]{1,0:T(4,128)}, u32[]{:S(2)}) %copy-start.1) | copy-done | bytes 408
  19.8 1.1 %shard_map.54 = s16[1,784,128]{2,1,0:T(8,128)(2,1)S(1)} custom-call(s32[1]{0:T(128)} %bitcast.me_ref, s32[32,1]{1,0:T(8,128)S(1)} %bitcast.3, f32[3,32]{1,0:T(4,128)S(1)} %copy-done.1, bf16[6,64,8192]{2,1,0:T(8,128)(2,1)S(1)} %copy-done), custom_call_target="tpu_custom_call" | custom-call | flops 1179648 | bytes 786432 | tf_op jit(solution)/shard_map/pallas_call | solution.py:229
  20.9 1.1 %shard_map.50 = s16[1,784,128]{2,1,0:T(8,128)(2,1)S(1)} custom-call(s32[1]{0:T(128)} %bitcast.me_ref, s32[32,1]{1,0:T(8,128)S(1)} %bitcast.4, f32[3,32]{1,0:T(4,128)S(1)} %copy-done.1, bf16[6,64,8192]{2,1,0:T(8,128)(2,1)S(1)} %copy-done), custom_call_target="tpu_custom_call" | custom-call | flops 1179648 | bytes 786432 | tf_op jit(solution)/shard_map/pallas_call | solution.py:229
  22.1 0.7 %collective-permute-start.11 = (s16[1,784,128]{2,1,0:T(8,128)(2,1)S(1)}, s16[1,784,128]{2,1,0:T(8,128)(2,1)S(1)}, u32[]{:S(2)}, u32[]{:S(2)}) collective-permute-start(s16[1,784,128]{2,1,0:T(8,128)(2,1)S(1)} %shard_map.54), channel_id=1, source_target_pairs={{0,8},{4,12},{8,0},{12,4},{16,24},{20,28},{24,16},{28,20},{1,9},{5... | collective-permute-start | bytes 602120 | tf_op jit(solution)/shard_map/ppermute | solution.py:329
  23.3 1.8 %shard_map.46 = (s16[1,784,128]{2,1,0:T(8,128)(2,1)S(1)}, s16[1,784,128]{2,1,0:T(8,128)(2,1)S(1)}, s16[1,784,128]{2,1,0:T(8,128)(2,1)S(1)}, s16[1,784,128]{2,1,0:T(8,128)(2,1)S(1)}) custom-call(s32[1]{0:T(128)} %bitcast.me_ref, s32[32,1]{1,0:T(8,128)S(1)} %bitcast.5, f32[3,32]{1,0:T(4,128)S(1)} %copy-done.1, bf16[6,64,8192]{2,1,0:T(8,128)(2,1)S(1)} %copy-done), custom_call_target="tpu_custom_call" | custom-call | flops 4718592 | bytes 3145728 | tf_op jit(solution)/shard_map/pallas_call | solution.py:229
  25.1 1.5 %collective-permute-start.2 = (s16[1,784,128]{2,1,0:T(8,128)(2,1)S(1)}, s16[1,784,128]{2,1,0:T(8,128)(2,1)S(1)}, u32[]{:S(2)}, u32[]{:S(2)}) collective-permute-start(s16[1,784,128]{2,1,0:T(8,128)(2,1)S(1)} %get-tuple-element.13), channel_id=1, source_target_pairs={{0,4},{4,0},{8,12},{12,8},{16,20},{20,16},{24,28},{28,24},{1,5},{5... | collective-permute-start | bytes 602120 | tf_op jit(solution)/shard_map/ppermute | solution.py:329
  26.6 1.4 %collective-permute-start.3 = (s16[1,784,128]{2,1,0:T(8,128)(2,1)S(1)}, s16[1,784,128]{2,1,0:T(8,128)(2,1)S(1)}, u32[]{:S(2)}, u32[]{:S(2)}) collective-permute-start(s16[1,784,128]{2,1,0:T(8,128)(2,1)S(1)} %get-tuple-element.14), channel_id=1, source_target_pairs={{0,8},{4,12},{8,0},{12,4},{16,24},{20,28},{24,16},{28,20},{1,9},{5... | collective-permute-start | bytes 602120 | tf_op jit(solution)/shard_map/ppermute | solution.py:329
  28.1 1.1 %shard_map.53 = s16[1,784,128]{2,1,0:T(8,128)(2,1)S(1)} custom-call(s32[1]{0:T(128)} %bitcast.me_ref, s32[32,1]{1,0:T(8,128)S(1)} %bitcast.6, f32[3,32]{1,0:T(4,128)S(1)} %copy-done.1, bf16[6,64,8192]{2,1,0:T(8,128)(2,1)S(1)} %copy-done), custom_call_target="tpu_custom_call" | custom-call | flops 1179648 | bytes 786432 | tf_op jit(solution)/shard_map/pallas_call | solution.py:229
  29.2 0.7 %collective-permute-start.10 = (s16[1,784,128]{2,1,0:T(8,128)(2,1)S(1)}, s16[1,784,128]{2,1,0:T(8,128)(2,1)S(1)}, u32[]{:S(2)}, u32[]{:S(2)}) collective-permute-start(s16[1,784,128]{2,1,0:T(8,128)(2,1)S(1)} %shard_map.53), channel_id=1, source_target_pairs={{0,8},{4,12},{8,0},{12,4},{16,24},{20,28},{24,16},{28,20},{1,9},{5... | collective-permute-start | bytes 602120 | tf_op jit(solution)/shard_map/ppermute | solution.py:329
  29.8 1.1 %shard_map.49 = s16[1,784,128]{2,1,0:T(8,128)(2,1)S(1)} custom-call(s32[1]{0:T(128)} %bitcast.me_ref, s32[32,1]{1,0:T(8,128)S(1)} %bitcast.7, f32[3,32]{1,0:T(4,128)S(1)} %copy-done.1, bf16[6,64,8192]{2,1,0:T(8,128)(2,1)S(1)} %copy-done), custom_call_target="tpu_custom_call" | custom-call | flops 1179648 | bytes 786432 | tf_op jit(solution)/shard_map/pallas_call | solution.py:229
  31.0 0.6 collective-permute-start.6
  31.6 1.2 %shard_map.55 = s16[1,784,128]{2,1,0:T(8,128)(2,1)S(1)} custom-call(s32[1]{0:T(128)} %bitcast.me_ref, s32[32,1]{1,0:T(8,128)S(1)} %bitcast.8, f32[3,32]{1,0:T(4,128)S(1)} %copy-done.1, bf16[6,64,8192]{2,1,0:T(8,128)(2,1)S(1)} %copy-done, s16[1,784,128]{2,1,0:T(8,128)(2,1)S(1)} %collective-permute-done.11.refs_0_), custom_call_target="tpu_custom_call" | custom-call | flops 1179648 | bytes 786432 | tf_op jit(solution)/shard_map/pallas_call | solution.py:229
  32.8 1.5 %collective-permute-start.12 = (s16[1,784,128]{2,1,0:T(8,128)(2,1)S(1)}, s16[1,784,128]{2,1,0:T(8,128)(2,1)S(1)}, u32[]{:S(2)}, u32[]{:S(2)}) collective-permute-start(s16[1,784,128]{2,1,0:T(8,128)(2,1)S(1)} %shard_map.55), channel_id=1, source_target_pairs={{0,4},{4,0},{8,12},{12,8},{16,20},{20,16},{24,28},{28,24},{1,5},{5... | collective-permute-start | bytes 602120 | tf_op jit(solution)/shard_map/ppermute | solution.py:329
  34.3 1.2 %shard_map.51 = s16[1,784,128]{2,1,0:T(8,128)(2,1)S(1)} custom-call(s32[1]{0:T(128)} %bitcast.me_ref, s32[32,1]{1,0:T(8,128)S(1)} %bitcast.9, f32[3,32]{1,0:T(4,128)S(1)} %copy-done.1, bf16[6,64,8192]{2,1,0:T(8,128)(2,1)S(1)} %copy-done, s16[1,784,128]{2,1,0:T(8,128)(2,1)S(1)} %collective-permute-done.7.refs_0_), custom_call_target="tpu_custom_call" | custom-call | flops 1179648 | bytes 786432 | tf_op jit(solution)/shard_map/pallas_call | solution.py:229
  35.5 1.5 %collective-permute-start.8 = (s16[1,784,128]{2,1,0:T(8,128)(2,1)S(1)}, s16[1,784,128]{2,1,0:T(8,128)(2,1)S(1)}, u32[]{:S(2)}, u32[]{:S(2)}) collective-permute-start(s16[1,784,128]{2,1,0:T(8,128)(2,1)S(1)} %shard_map.51), channel_id=1, source_target_pairs={{0,8},{4,12},{8,0},{12,4},{16,24},{20,28},{24,16},{28,20},{1,9},{5... | collective-permute-start | bytes 602120 | tf_op jit(solution)/shard_map/ppermute | solution.py:329
  37.6 1.4 %shard_map.47 = (s16[1,784,128]{2,1,0:T(8,128)(2,1)S(1)}, s16[1,784,128]{2,1,0:T(8,128)(2,1)S(1)}) custom-call(s32[1]{0:T(128)} %bitcast.me_ref, s32[32,1]{1,0:T(8,128)S(1)} %bitcast.10, f32[3,32]{1,0:T(4,128)S(1)} %copy-done.1, bf16[6,64,8192]{2,1,0:T(8,128)(2,1)S(1)} %copy-done, s16[1,784,128]{2,1,0:T(8,128)(2,1)S(1)} %collective-permute-done.2.refs_0_, ...), custom_call_target="tpu_custom_call" | custom-call | flops 2359296 | bytes 1572864 | tf_op jit(solution)/shard_map/pallas_call | solution.py:229
  39.0 0.6 collective-permute-start.1
  39.7 1.4 %collective-permute-start.4 = (s16[1,784,128]{2,1,0:T(8,128)(2,1)S(1)}, s16[1,784,128]{2,1,0:T(8,128)(2,1)S(1)}, u32[]{:S(2)}, u32[]{:S(2)}) collective-permute-start(s16[1,784,128]{2,1,0:T(8,128)(2,1)S(1)} %get-tuple-element.15), channel_id=1, source_target_pairs={{0,8},{4,12},{8,0},{12,4},{16,24},{20,28},{24,16},{28,20},{1,9},{5... | collective-permute-start | bytes 602120 | tf_op jit(solution)/shard_map/ppermute | solution.py:329
  41.1 2.3 %collective-permute-done.12.refs_1_ = s16[1,784,128]{2,1,0:T(8,128)(2,1)S(1)} collective-permute-done((s16[1,784,128]{2,1,0:T(8,128)(2,1)S(1)}, s16[1,784,128]{2,1,0:T(8,128)(2,1)S(1)}, u32[]{:S(2)}, u32[]{:S(2)}) %collective-permute-start.12) | collective-permute-done | bytes 200736 | tf_op jit(solution)/shard_map/ppermute | solution.py:329
  43.9 1.2 %shard_map.56 = s16[1,784,128]{2,1,0:T(8,128)(2,1)S(1)} custom-call(s32[1]{0:T(128)} %bitcast.me_ref, s32[32,1]{1,0:T(8,128)S(1)} %bitcast.11, f32[3,32]{1,0:T(4,128)S(1)} %copy-done.1, bf16[6,64,8192]{2,1,0:T(8,128)(2,1)S(1)} %copy-done, s16[1,784,128]{2,1,0:T(8,128)(2,1)S(1)} %collective-permute-done.10.refs_0_, ...), custom_call_target="tpu_custom_call" | custom-call | flops 1179648 | bytes 786432 | tf_op jit(solution)/shard_map/pallas_call | solution.py:229
  45.8 1.2 %shard_map.52 = s16[1,784,128]{2,1,0:T(8,128)(2,1)S(1)} custom-call(s32[1]{0:T(128)} %bitcast.me_ref, s32[32,1]{1,0:T(8,128)S(1)} %bitcast.12, f32[3,32]{1,0:T(4,128)S(1)} %copy-done.1, bf16[6,64,8192]{2,1,0:T(8,128)(2,1)S(1)} %copy-done, s16[1,784,128]{2,1,0:T(8,128)(2,1)S(1)} %collective-permute-done.6.refs_0_, ...), custom_call_target="tpu_custom_call" | custom-call | flops 1179648 | bytes 786432 | tf_op jit(solution)/shard_map/pallas_call | solution.py:229
  47.0 0.7 %collective-permute-done.refs_0_ = s16[1,784,128]{2,1,0:T(8,128)(2,1)S(1)} collective-permute-done((s16[1,784,128]{2,1,0:T(8,128)(2,1)S(1)}, s16[1,784,128]{2,1,0:T(8,128)(2,1)S(1)}, u32[]{:S(2)}, u32[]{:S(2)}) %collective-permute-start) | collective-permute-done | bytes 200736 | tf_op jit(solution)/shard_map/ppermute | solution.py:329
  47.7 1.8 %collective-permute-start.9 = (s16[1,784,128]{2,1,0:T(8,128)(2,1)S(1)}, s16[1,784,128]{2,1,0:T(8,128)(2,1)S(1)}, u32[]{:S(2)}, u32[]{:S(2)}) collective-permute-start(s16[1,784,128]{2,1,0:T(8,128)(2,1)S(1)} %shard_map.52), channel_id=1, source_target_pairs={{0,16},{4,20},{8,24},{12,28},{16,0},{20,4},{24,8},{28,12},{1,17},{... | collective-permute-start | bytes 602120 | tf_op jit(solution)/shard_map/ppermute | solution.py:329
  49.4 1.8 %collective-permute-done.1.refs_1_ = s16[1,784,128]{2,1,0:T(8,128)(2,1)S(1)} collective-permute-done((s16[1,784,128]{2,1,0:T(8,128)(2,1)S(1)}, s16[1,784,128]{2,1,0:T(8,128)(2,1)S(1)}, u32[]{:S(2)}, u32[]{:S(2)}) %collective-permute-start.1) | collective-permute-done | bytes 200736 | tf_op jit(solution)/shard_map/ppermute | solution.py:329
  51.3 3.2 %collective-permute-done.4.refs_2_ = s16[1,784,128]{2,1,0:T(8,128)(2,1)S(1)} collective-permute-done((s16[1,784,128]{2,1,0:T(8,128)(2,1)S(1)}, s16[1,784,128]{2,1,0:T(8,128)(2,1)S(1)}, u32[]{:S(2)}, u32[]{:S(2)}) %collective-permute-start.4) | collective-permute-done | bytes 200736 | tf_op jit(solution)/shard_map/ppermute | solution.py:329
  54.5 1.4 %shard_map.48.held_ref = f32[3,64,1024]{2,1,0:T(8,128)S(1)} custom-call(s32[1]{0:T(128)} %bitcast.me_ref, s32[32,1]{1,0:T(8,128)S(1)} %bitcast.13, f32[3,32]{1,0:T(4,128)S(1)} %copy-done.1, bf16[6,64,8192]{2,1,0:T(8,128)(2,1)S(1)} %copy-done, s16[1,784,128]{2,1,0:T(8,128)(2,1)S(1)} %collective-permute-done.refs_0_, ...), custom_call_target="tpu_custom_call" | custom-call | flops 2359296 | bytes 1572864 | tf_op jit(solution)/shard_map/pallas_call | solution.py:253
  55.9 5.5 %collective-permute-done.13.refs_1_ = s16[1,784,128]{2,1,0:T(8,128)(2,1)S(1)} collective-permute-done((s16[1,784,128]{2,1,0:T(8,128)(2,1)S(1)}, s16[1,784,128]{2,1,0:T(8,128)(2,1)S(1)}, u32[]{:S(2)}, u32[]{:S(2)}) %collective-permute-start.13) | collective-permute-done | bytes 200736 | tf_op jit(solution)/shard_map/ppermute | solution.py:329
  61.4 2.1 %collective-permute-done.9.refs_0_ = s16[1,784,128]{2,1,0:T(8,128)(2,1)S(1)} collective-permute-done((s16[1,784,128]{2,1,0:T(8,128)(2,1)S(1)}, s16[1,784,128]{2,1,0:T(8,128)(2,1)S(1)}, u32[]{:S(2)}, u32[]{:S(2)}) %collective-permute-start.9) | collective-permute-done | bytes 200736 | tf_op jit(solution)/shard_map/ppermute | solution.py:329
  63.5 0.9 %shard_map.57 = bf16[3,64,1024]{2,1,0:T(8,128)(2,1)} custom-call(f32[3,64,1024]{2,1,0:T(8,128)S(1)} %shard_map.48.held_ref, s16[1,784,128]{2,1,0:T(8,128)(2,1)S(1)} %collective-permute-done.9.refs_0_, s16[1,784,128]{2,1,0:T(8,128)(2,1)S(1)} %collective-permute-done.13.refs_1_), custom_call_target="tpu_custom_call" | custom-call | flops 786432 | bytes 1572864 | tf_op jit(solution)/shard_map/pallas_call | solution.py:261
  (15 shorter events, 2.9 us)
Async XLA Ops:
  1.9 14.4 %all-to-all-start = ((s32[32,1,1]{2,1,0:T(1,128)}), s32[32,1,1]{2,1,0:T(1,128)S(1)}, u32[]{:S(2)}, u32[]{:S(2)}) async-start(s32[32,1,1]{2,1,0:T(1,128)} %broadcast_in_dim.9), calls=%async_computation | async-start | bytes 32768 | tf_op jit(solution)/shard_map/all_to_all | solution.py:314
  16.3 2.8 %copy-start = (bf16[6,64,8192]{2,1,0:T(8,128)(2,1)S(1)}, bf16[6,64,8192]{2,1,0:T(8,128)(2,1)}, u32[]{:S(2)}) copy-start(bf16[6,64,8192]{2,1,0:T(8,128)(2,1)} %x_ref.21) | copy-start | bytes 18874372
  19.1 0.7 %copy-start.1 = (f32[3,32]{1,0:T(4,128)S(1)}, f32[3,32]{1,0:T(4,128)}, u32[]{:S(2)}) copy-start(f32[3,32]{1,0:T(4,128)} %coef_ref.21) | copy-start | bytes 1156
  22.1 8.9 %collective-permute-start.11 = (s16[1,784,128]{2,1,0:T(8,128)(2,1)S(1)}, s16[1,784,128]{2,1,0:T(8,128)(2,1)S(1)}, u32[]{:S(2)}, u32[]{:S(2)}) collective-permute-start(s16[1,784,128]{2,1,0:T(8,128)(2,1)S(1)} %shard_map.54), channel_id=1, source_target_pairs={{0,8},{4,12},{8,0},{12,4},{16,24},{20,28},{24,16},{28,20},{1,9},{5... | collective-permute-start | bytes 602120 | tf_op jit(solution)/shard_map/ppermute | solution.py:329
  22.7 10.0 %collective-permute-start.7 = (s16[1,784,128]{2,1,0:T(8,128)(2,1)S(1)}, s16[1,784,128]{2,1,0:T(8,128)(2,1)S(1)}, u32[]{:S(2)}, u32[]{:S(2)}) collective-permute-start(s16[1,784,128]{2,1,0:T(8,128)(2,1)S(1)} %shard_map.50), channel_id=1, source_target_pairs={{0,4},{4,0},{8,12},{12,8},{16,20},{20,16},{24,28},{28,24},{1,5},{5... | collective-permute-start | bytes 602120 | tf_op jit(solution)/shard_map/ppermute | solution.py:329
  25.1 10.4 %collective-permute-start.2 = (s16[1,784,128]{2,1,0:T(8,128)(2,1)S(1)}, s16[1,784,128]{2,1,0:T(8,128)(2,1)S(1)}, u32[]{:S(2)}, u32[]{:S(2)}) collective-permute-start(s16[1,784,128]{2,1,0:T(8,128)(2,1)S(1)} %get-tuple-element.13), channel_id=1, source_target_pairs={{0,4},{4,0},{8,12},{12,8},{16,20},{20,16},{24,28},{28,24},{1,5},{5... | collective-permute-start | bytes 602120 | tf_op jit(solution)/shard_map/ppermute | solution.py:329
  26.6 10.4 %collective-permute-start.3 = (s16[1,784,128]{2,1,0:T(8,128)(2,1)S(1)}, s16[1,784,128]{2,1,0:T(8,128)(2,1)S(1)}, u32[]{:S(2)}, u32[]{:S(2)}) collective-permute-start(s16[1,784,128]{2,1,0:T(8,128)(2,1)S(1)} %get-tuple-element.14), channel_id=1, source_target_pairs={{0,8},{4,12},{8,0},{12,4},{16,24},{20,28},{24,16},{28,20},{1,9},{5... | collective-permute-start | bytes 602120 | tf_op jit(solution)/shard_map/ppermute | solution.py:329
  29.2 9.8 %collective-permute-start.10 = (s16[1,784,128]{2,1,0:T(8,128)(2,1)S(1)}, s16[1,784,128]{2,1,0:T(8,128)(2,1)S(1)}, u32[]{:S(2)}, u32[]{:S(2)}) collective-permute-start(s16[1,784,128]{2,1,0:T(8,128)(2,1)S(1)} %shard_map.53), channel_id=1, source_target_pairs={{0,8},{4,12},{8,0},{12,4},{16,24},{20,28},{24,16},{28,20},{1,9},{5... | collective-permute-start | bytes 602120 | tf_op jit(solution)/shard_map/ppermute | solution.py:329
  31.0 8.7 %collective-permute-start.6 = (s16[1,784,128]{2,1,0:T(8,128)(2,1)S(1)}, s16[1,784,128]{2,1,0:T(8,128)(2,1)S(1)}, u32[]{:S(2)}, u32[]{:S(2)}) collective-permute-start(s16[1,784,128]{2,1,0:T(8,128)(2,1)S(1)} %shard_map.49), channel_id=1, source_target_pairs={{0,4},{4,0},{8,12},{12,8},{16,20},{20,16},{24,28},{28,24},{1,5},{5... | collective-permute-start | bytes 602120 | tf_op jit(solution)/shard_map/ppermute | solution.py:329
  32.8 10.6 %collective-permute-start.12 = (s16[1,784,128]{2,1,0:T(8,128)(2,1)S(1)}, s16[1,784,128]{2,1,0:T(8,128)(2,1)S(1)}, u32[]{:S(2)}, u32[]{:S(2)}) collective-permute-start(s16[1,784,128]{2,1,0:T(8,128)(2,1)S(1)} %shard_map.55), channel_id=1, source_target_pairs={{0,4},{4,0},{8,12},{12,8},{16,20},{20,16},{24,28},{28,24},{1,5},{5... | collective-permute-start | bytes 602120 | tf_op jit(solution)/shard_map/ppermute | solution.py:329
  35.5 9.7 %collective-permute-start.8 = (s16[1,784,128]{2,1,0:T(8,128)(2,1)S(1)}, s16[1,784,128]{2,1,0:T(8,128)(2,1)S(1)}, u32[]{:S(2)}, u32[]{:S(2)}) collective-permute-start(s16[1,784,128]{2,1,0:T(8,128)(2,1)S(1)} %shard_map.51), channel_id=1, source_target_pairs={{0,8},{4,12},{8,0},{12,4},{16,24},{20,28},{24,16},{28,20},{1,9},{5... | collective-permute-start | bytes 602120 | tf_op jit(solution)/shard_map/ppermute | solution.py:329
  37.0 10.7 %collective-permute-start = (s16[1,784,128]{2,1,0:T(8,128)(2,1)S(1)}, s16[1,784,128]{2,1,0:T(8,128)(2,1)S(1)}, u32[]{:S(2)}, u32[]{:S(2)}) collective-permute-start(s16[1,784,128]{2,1,0:T(8,128)(2,1)S(1)} %get-tuple-element.11), channel_id=1, source_target_pairs={{0,4},{4,0},{8,12},{12,8},{16,20},{20,16},{24,28},{28,24},{1,5},{5... | collective-permute-start | bytes 602120 | tf_op jit(solution)/shard_map/ppermute | solution.py:329
  39.0 12.2 %collective-permute-start.1 = (s16[1,784,128]{2,1,0:T(8,128)(2,1)S(1)}, s16[1,784,128]{2,1,0:T(8,128)(2,1)S(1)}, u32[]{:S(2)}, u32[]{:S(2)}) collective-permute-start(s16[1,784,128]{2,1,0:T(8,128)(2,1)S(1)} %get-tuple-element.12), channel_id=1, source_target_pairs={{0,8},{4,12},{8,0},{12,4},{16,24},{20,28},{24,16},{28,20},{1,9},{5... | collective-permute-start | bytes 602120 | tf_op jit(solution)/shard_map/ppermute | solution.py:329
  39.7 14.8 %collective-permute-start.4 = (s16[1,784,128]{2,1,0:T(8,128)(2,1)S(1)}, s16[1,784,128]{2,1,0:T(8,128)(2,1)S(1)}, u32[]{:S(2)}, u32[]{:S(2)}) collective-permute-start(s16[1,784,128]{2,1,0:T(8,128)(2,1)S(1)} %get-tuple-element.15), channel_id=1, source_target_pairs={{0,8},{4,12},{8,0},{12,4},{16,24},{20,28},{24,16},{28,20},{1,9},{5... | collective-permute-start | bytes 602120 | tf_op jit(solution)/shard_map/ppermute | solution.py:329
  43.4 11.1 %collective-permute-start.5 = (s16[1,784,128]{2,1,0:T(8,128)(2,1)S(1)}, s16[1,784,128]{2,1,0:T(8,128)(2,1)S(1)}, u32[]{:S(2)}, u32[]{:S(2)}) collective-permute-start(s16[1,784,128]{2,1,0:T(8,128)(2,1)S(1)} %get-tuple-element.16), channel_id=1, source_target_pairs={{0,4},{4,0},{8,12},{12,8},{16,20},{20,16},{24,28},{28,24},{1,5},{5... | collective-permute-start | bytes 602120 | tf_op jit(solution)/shard_map/ppermute | solution.py:329
  45.1 16.2 %collective-permute-start.13 = (s16[1,784,128]{2,1,0:T(8,128)(2,1)S(1)}, s16[1,784,128]{2,1,0:T(8,128)(2,1)S(1)}, u32[]{:S(2)}, u32[]{:S(2)}) collective-permute-start(s16[1,784,128]{2,1,0:T(8,128)(2,1)S(1)} %shard_map.56), channel_id=1, source_target_pairs={{0,16},{4,20},{8,24},{12,28},{16,0},{20,4},{24,8},{28,12},{1,17},{... | collective-permute-start | bytes 602120 | tf_op jit(solution)/shard_map/ppermute | solution.py:329
  47.7 15.9 %collective-permute-start.9 = (s16[1,784,128]{2,1,0:T(8,128)(2,1)S(1)}, s16[1,784,128]{2,1,0:T(8,128)(2,1)S(1)}, u32[]{:S(2)}, u32[]{:S(2)}) collective-permute-start(s16[1,784,128]{2,1,0:T(8,128)(2,1)S(1)} %shard_map.52), channel_id=1, source_target_pairs={{0,16},{4,20},{8,24},{12,28},{16,0},{20,4},{24,8},{28,12},{1,17},{... | collective-permute-start | bytes 602120 | tf_op jit(solution)/shard_map/ppermute | solution.py:329

commit v2 on v1

--- a/solution.py
+++ b/solution.py
@@ -11,6 +11,7 @@
 LANES = 128
 TALL = 16
 VMEM_LIMIT = 24 * 1024 * 1024
+PACK_LIMIT = 58 * 1024 * 1024
 TOP = 32600.0
 STEPS = 64.0
 LN2 = 0.6931471805599453
@@ -148,38 +149,57 @@
             lax.fori_loop(0, size, one, 0)
 
 
-def held_kernel(group, flows, plan, kinds, me_ref, table_ref, coef_ref, x_ref, *refs):
-    bits = len(flows[0][2])
-    *inputs, held_ref = refs
+def pack_kernel(flow, me_ref, x_ref, out_ref, sem):
+    first, height, order = flow
+    width = x_ref.shape[2] >> len(order)
+    dest = me_ref[0] ^ (1 << order[0])
+    cols = pl.ds(pl.multiple_of(dest * width, LANES), width)
+    copy = pltpu.make_async_copy(x_ref.at[:, pl.ds(first, height), cols], out_ref.at[0], sem)
+    copy.start()
+    copy.wait()
+
+
+def held_kernel(group, flow, base, kinds, me_ref, table_ref, coef_ref, x_ref, piece_ref, held_ref):
+    first, height, order = flow
     me = me_ref[0]
     w = weights_of(me, group, table_ref, coef_ref, x_ref.shape[0])
-    width = x_ref.shape[2] >> bits
+    width = x_ref.shape[2] >> len(order)
+    tiles = tiles_of(height, width)
+    block = piece_ref.at[base]
+    raw = len(block.shape) == 3
+    if raw:
+        other = weights_of(me ^ (1 << order[0]), group, table_ref, coef_ref, x_ref.shape[0])
+        received = []
+    else:
+        received = [(block, scales_of(block, len(tiles), kinds))]
+    for t, (row, c) in enumerate(tiles):
+        rows, place = pl.ds(row, TALL), pl.ds(c, LANES)
+        cols = pl.ds(pl.multiple_of(me * width + c, LANES), LANES)
+        sources = [(w, x_ref, pl.ds(first + row, TALL), cols)]
+        if raw:
+            sources.append((other, block, rows, place))
+        accs = tile_sums(sources, received, len(tiles), t)
+        for k in range(kinds):
+            held_ref[k, rows, place] = accs[k]
+
+
+def last_kernel(flows, kinds, *refs):
+    *inputs, out_ref = refs
+    helds, inputs = inputs[: len(flows)], inputs[len(flows) :]
+    width = out_ref.shape[2]
     for f, (first, height, _) in enumerate(flows):
+        held_ref = helds[f]
         tiles = tiles_of(height, width)
-        blocks = [inputs[at * len(flows) + f].at[base] for at, base in plan[0]]
-        received = [(b, scales_of(b, len(tiles), kinds)) for b in blocks]
-        for t, (row, c) in enumerate(tiles):
-            rows = pl.ds(first + row, TALL)
-            cols = pl.ds(pl.multiple_of(me * width + c, LANES), LANES)
-            accs = tile_sums([(w, x_ref, rows, cols)], received, len(tiles), t)
-            for k in range(kinds):
-                held_ref[k, rows, c : c + LANES] = accs[k]
-
-
-def last_kernel(flows, kinds, held_ref, *refs):
-    *inputs, out_ref = refs
-    width = held_ref.shape[2]
-    for (first, height, _), ref in zip(flows, inputs):
-        tiles = tiles_of(height, width)
-        block = ref.at[0]
-        scales = scales_of(block, len(tiles), kinds)
+        blocks = [ref.at[0] for ref in inputs[f :: len(flows)]]
+        scales = [scales_of(block, len(tiles), kinds) for block in blocks]
         for t, (row, c) in enumerate(tiles):
             for k in range(kinds):
-                at = (pl.ds(first + row, TALL), slice(c, c + LANES))
-                code = block[pl.ds((k * len(tiles) + t) * TALL, TALL), :]
-                code = code.astype(jnp.int32).astype(jnp.float32)
-                total = held_ref[(k, *at)] + code * scales[k]
-                out_ref[(k, *at)] = total.astype(jnp.bfloat16)
+                total = held_ref[k, row : row + TALL, c : c + LANES]
+                for block, scale in zip(blocks, scales):
+                    code = block[pl.ds((k * len(tiles) + t) * TALL, TALL), :]
+                    total = total + code.astype(jnp.int32).astype(jnp.float32) * scale[k]
+                rows = slice(first + row, first + row + TALL)
+                out_ref[k, rows, c : c + LANES] = total.astype(jnp.bfloat16)
 
 
 def block_rows(flow, kinds, width):
@@ -188,6 +208,7 @@
 
 SMEM = pl.BlockSpec(memory_space=pltpu.SMEM)
 VMEM = pl.BlockSpec(memory_space=pltpu.VMEM)
+ANY = pl.BlockSpec(memory_space=pl.ANY)
 PARAMS = pltpu.CompilerParams(vmem_limit_bytes=VMEM_LIMIT)
 
 
@@ -195,6 +216,20 @@
     return pl.CostEstimate(
         flops=2 * slots * elements, bytes_accessed=8 * elements, transcendentals=0
     )
+
+
+def pack_call(flow, me, x):
+    width = x.shape[2] >> len(flow[2])
+    shape = (1, x.shape[0], flow[1], width)
+    return pl.pallas_call(
+        functools.partial(pack_kernel, flow),
+        in_specs=[SMEM, ANY],
+        out_specs=VMEM,
+        out_shape=jax.ShapeDtypeStruct(shape, x.dtype),
+        scratch_shapes=[pltpu.SemaphoreType.DMA],
+        compiler_params=pltpu.CompilerParams(vmem_limit_bytes=PACK_LIMIT),
+        cost_estimate=cost(x.size >> 4, 1),
+    )(me, x)
 
 
 def gather_plan(chosen, bits, stage, launch, arrived, until):
@@ -242,65 +277,78 @@
     }
 
 
-def last_calls(flows, group, me, table, coef, x, arrived):
-    bits = len(flows[0][2])
+def held_call(flow, f, group, me, table, coef, x, arrived):
+    bits = len(flow[2])
     kinds = coef.shape[0]
     width = x.shape[2] >> bits
-    chosen = tuple(range(len(flows)))
-    arrays, plan = gather_plan(chosen, bits, bits, [()], arrived, bits - 1)
-    shape = (kinds, x.shape[1], width)
-    elements = kinds * x.shape[1] * width
-    held = pl.pallas_call(
-        functools.partial(held_kernel, group, flows, plan, kinds),
-        in_specs=[SMEM, SMEM, SMEM, VMEM] + [VMEM] * len(arrays),
+    found, base = source_of(0, bits, (), bits)
+    return pl.pallas_call(
+        functools.partial(held_kernel, group, flow, base, kinds),
+        in_specs=[SMEM, SMEM, SMEM, VMEM, VMEM],
         out_specs=VMEM,
-        out_shape=jax.ShapeDtypeStruct(shape, jnp.float32),
+        out_shape=jax.ShapeDtypeStruct((kinds, flow[1], width), jnp.float32),
         compiler_params=PARAMS,
-        cost_estimate=cost(elements, x.shape[0]),
-    )(me, table, coef, x, *arrays)
+        cost_estimate=cost(kinds * flow[1] * width, x.shape[0]),
+    )(me, table, coef, x, arrived[0, found, f])
+
+
+def last_call(flows, x, helds, arrived):
+    bits = len(flows[0][2])
+    kinds = helds[0].shape[0]
+    shape = (kinds, x.shape[1], x.shape[2] >> bits)
+    arrays = [
+        arrived[earlier, source_of(earlier, bits, (), bits)[0], f]
+        for earlier in range(1, bits)
+        for f in range(len(flows))
+    ]
     return pl.pallas_call(
         functools.partial(last_kernel, flows, kinds),
-        in_specs=[VMEM] * (1 + len(flows)),
+        in_specs=[VMEM] * (len(flows) + len(arrays)),
         out_specs=VMEM,
         out_shape=jax.ShapeDtypeStruct(shape, jnp.bfloat16),
         compiler_params=PARAMS,
-        cost_estimate=cost(elements, 2),
-    )(held, *[arrived[bits - 1, (), f] for f in chosen])
+        cost_estimate=cost(kinds * x.shape[1] * shape[2], 2),
+    )(*helds, *arrays)
 
 
 def schedule_of(bits):
     make, move = (lambda *a: ("make", a)), (lambda *a: ("move", a))
+    hold = lambda f: ("hold", f)
     if bits == 3:
-        steps = []
-        for stage, pattern, f in (
-            (0, (1, 1), 0),
-            (0, (1, 1), 1),
-            (0, (0, 1), 0),
-            (1, (1,), 0),
-            (0, (0, 1), 1),
-            (1, (1,), 1),
-        ):
-            steps += [make(stage, (pattern,), (f,)), move(stage, pattern, f)]
-        return steps + [
-            make(0, ((1, 0), (0, 0)), (0, 1)),
+        return [
+            make(0, ((1, 1),), (0, 1)),
+            move(0, (1, 1), 0),
+            move(0, (1, 1), 1),
+            make(0, ((0, 1),), (0,)),
+            move(0, (0, 1), 0),
+            make(0, ((0, 1),), (1,)),
+            make(1, ((1,),), (0,)),
+            move(1, (1,), 0),
+            move(0, (0, 1), 1),
+            make(1, ((1,),), (1,)),
+            move(1, (1,), 1),
+            make(0, ((1, 0), (0, 0)), (0,)),
+            move(0, (1, 0), 0),
             make(2, ((),), (0,)),
             move(2, (), 0),
-            move(0, (1, 0), 0),
+            make(0, ((1, 0),), (1,)),
             move(0, (1, 0), 1),
+            move(0, (0, 0), 0),
             make(2, ((),), (1,)),
             move(2, (), 1),
-            move(0, (0, 0), 0),
-            move(0, (0, 0), 1),
-            make(1, ((0,),), (0, 1)),
+            hold(1),
+            make(1, ((0,),), (0,)),
             move(1, (0,), 0),
+            make(1, ((0,),), (1,)),
             move(1, (0,), 1),
+            hold(0),
         ]
     steps = []
     for stage in range(bits):
         for pattern in patterns_of(stage, bits):
             steps.append(make(stage, (pattern,), (0, 1)))
             steps += [move(stage, pattern, f) for f in (0, 1)]
-    return steps
+    return steps + [hold(0), hold(1)]
 
 
 def on_device(snapshots, counts, order, coefficients):
@@ -312,9 +360,17 @@
     me = lax.axis_index("snap").reshape(1)
     own = (order << COUNT_BITS) + counts
     table = lax.all_to_all(
-        jnp.broadcast_to(own[:, None], (owners * group, 1)), ("snap", "row"), 0, 0, tiled=True
+        jnp.broadcast_to(own[:, None], (owners * group, 1)),
+        ("snap", "row"),
+        0,
+        0,
+        tiled=True,
     )
-    made, arrived = {}, {}
+    made, arrived, helds = {}, {}, {}
+    if bits == 3:
+        raw = pack_call(flows[1], me, snapshots)
+        pairs = [(d, d ^ (1 << flows[1][2][0])) for d in range(owners)]
+        arrived[0, (0, 0), 1] = lax.ppermute(raw, "snap", pairs)
     for kind, step in schedule_of(bits):
         if kind == "make":
             stage, launch, chosen = step
@@ -323,11 +379,15 @@
                 snapshots, arrived,
             )
             made.update({(stage, *key): value for key, value in sent.items()})
+        elif kind == "hold":
+            helds[step] = held_call(
+                flows[step], step, group, me, table, coefficients, snapshots, arrived
+            )
         else:
             stage, _, f = step
             pairs = [(d, d ^ (1 << flows[f][2][stage])) for d in range(owners)]
             arrived[step] = lax.ppermute(made[step], "snap", pairs)
-    return last_calls(flows, group, me, table, coefficients, snapshots, arrived)
+    return last_call(flows, snapshots, [helds[f] for f in range(len(flows))], arrived)
 
 
 def solution(mesh):

time: 64.6 us -> 67.7 us (1.048)
  waiting for transfers between devices: 22.8 us -> 17.8 us
  Pallas kernels: 14.7 us -> 18.1 us
  local copies, waits for them, and re-layouts: 4.08 us -> 6.87 us
  starting transfers between devices: 21.5 us -> 23.1 us
    ppermute x14 -> x13, waiting for transfers between devices: 15.7 us -> 7.53 us  [on_device(): arrived[step] = lax.ppermute(made[step], 'snap', pairs)]
    ppermute x0 -> x1, waiting for transfers between devices: none -> 3.16 us  [on_device(): arrived[0, (0, 0), 1] = lax.ppermute(raw, 'snap', pairs)]
    pallas_call x2 -> x4, Pallas kernels: 2.27 us -> 5.09 us  [the longest x2 2.36 us: held_call(): pl.pallas_call(functools.partial(held_kernel, group, flow, base, kinds),...]
    unnamed x4 -> x8, local copies, waits for them, and re-layouts: 3.47 us -> 6.26 us
    ppermute x14 -> x13, starting transfers between devices: 14.1 us -> 15.1 us  [on_device(): arrived[step] = lax.ppermute(made[step], 'snap', pairs)]
    ppermute x0 -> x1, starting transfers between devices: none -> 0.68 us  [on_device(): arrived[0, (0, 0), 1] = lax.ppermute(raw, 'snap', pairs)]
    pallas_call x10 -> x11, Pallas kernels: 12.4 us -> 13 us  [send_call(): pl.pallas_call(functools.partial(send_kernel, group, mine, stage, launch,...]
  transfers between devices with their start and end apart: 15 -> 15, of which waited for: 7 -> 5; matrix products, arithmetic and copies ran while one was open for 0% -> 0% of each run, Pallas kernels for 18% -> 23%
where the time goes in v2:
time: 67.7 us; the launch traced here: 67.4 us
  starting transfers between devices  23.1 us (34%)
  Pallas kernels  18.1 us (27%)
  waiting for transfers between devices  17.8 us (26%)
  local copies, waits for them, and re-layouts  6.87 us (10%)
  between operations  1.47 us (2%)
    ppermute x13, starting transfers between devices, on_device(): arrived[step] = lax.ppermute(made[step], 'snap', pairs)  15.1 us
    pallas_call x11, Pallas kernels, send_call(): pl.pallas_call(functools.partial(send_kernel, group, mine, stage, launch,...  13 us
    ppermute x13, waiting for transfers between devices, on_device(): arrived[step] = lax.ppermute(made[step], 'snap', pairs)  7.53 us
    all_to_all x1, starting transfers between devices, on_device(): lax.all_to_all(jnp.broadcast_to(own[:, None], (owners * group, 1)), ('sna...  7.33 us
    all_to_all x1, waiting for transfers between devices, on_device(): lax.all_to_all(jnp.broadcast_to(own[:, None], (owners * group, 1)), ('sna...  7.1 us
    unnamed x8, local copies, waits for them, and re-layouts  6.26 us
    ppermute x1, waiting for transfers between devices, on_device(): arrived[0, (0, 0), 1] = lax.ppermute(raw, 'snap', pairs)  3.16 us
    pallas_call x2, Pallas kernels, held_call(): pl.pallas_call(functools.partial(held_kernel, group, flow, base, kinds),...  2.36 us
  transfers between devices with their start and end apart: 15, of which 5 were waited for; matrix products, arithmetic and copies ran while one was open for 0% of the time, Pallas kernels for 23%

profile of v2, /device:TPU:0, one launch (start us, length us, event | category | flops | bytes accessed | tf_op | source)
XLA Modules:
  0.0 67.4 jit_solution(1974935932208364936)
XLA Ops:
  1.9 7.3 %all-to-all-start = ((s32[32,1,1]{2,1,0:T(1,128)}), s32[32,1,1]{2,1,0:T(1,128)S(1)}, u32[]{:S(2)}, u32[]{:S(2)}) async-start(s32[32,1,1]{2,1,0:T(1,128)} %broadcast_in_dim.9), calls=%async_computation | async-start | bytes 32768 | tf_op jit(solution)/shard_map/all_to_all | solution.py:362
  9.3 7.1 %all-to-all-done = s32[32,1,1]{2,1,0:T(1,128)S(1)} async-done(((s32[32,1,1]{2,1,0:T(1,128)}), s32[32,1,1]{2,1,0:T(1,128)S(1)}, u32[]{:S(2)}, u32[]{:S(2)}) %all-to-all-start) | async-done | bytes 160 | tf_op jit(solution)/shard_map/all_to_all | solution.py:362
  16.4 2.8 %copy-done = bf16[6,64,8192]{2,1,0:T(8,128)(2,1)S(1)} copy-done((bf16[6,64,8192]{2,1,0:T(8,128)(2,1)S(1)}, bf16[6,64,8192]{2,1,0:T(8,128)(2,1)}, u32[]{:S(2)}) %copy-start) | copy-done | bytes 6291480
  19.8 1.3 %shard_map.54 = (s16[1,784,128]{2,1,0:T(8,128)(2,1)S(1)}, s16[1,784,128]{2,1,0:T(8,128)(2,1)S(1)}) custom-call(s32[1]{0:T(128)} %bitcast.me_ref, s32[32,1]{1,0:T(8,128)S(1)} %bitcast.3, f32[3,32]{1,0:T(4,128)S(1)} %copy-done.2, bf16[6,64,8192]{2,1,0:T(8,128)(2,1)S(1)} %copy-done), custom_call_target="tpu_custom_call" | custom-call | flops 2359296 | bytes 1572864 | tf_op jit(solution)/shard_map/pallas_call | solution.py:264
  22.4 1.1 %shard_map.51 = s16[1,784,128]{2,1,0:T(8,128)(2,1)S(1)} custom-call(s32[1]{0:T(128)} %bitcast.me_ref, s32[32,1]{1,0:T(8,128)S(1)} %bitcast.4, f32[3,32]{1,0:T(4,128)S(1)} %copy-done.2, bf16[6,64,8192]{2,1,0:T(8,128)(2,1)S(1)} %copy-done), custom_call_target="tpu_custom_call" | custom-call | flops 1179648 | bytes 786432 | tf_op jit(solution)/shard_map/pallas_call | solution.py:264
  23.5 1.5 %collective-permute-start.4 = (s16[1,784,128]{2,1,0:T(8,128)(2,1)S(1)}, s16[1,784,128]{2,1,0:T(8,128)(2,1)S(1)}, u32[]{:S(2)}, u32[]{:S(2)}) collective-permute-start(s16[1,784,128]{2,1,0:T(8,128)(2,1)S(1)} %shard_map.51), channel_id=1, source_target_pairs={{0,8},{4,12},{8,0},{12,4},{16,24},{20,28},{24,16},{28,20},{1,9},{5... | collective-permute-start | bytes 602120 | tf_op jit(solution)/shard_map/ppermute | solution.py:389
  25.0 1.1 %shard_map.53 = s16[1,784,128]{2,1,0:T(8,128)(2,1)S(1)} custom-call(s32[1]{0:T(128)} %bitcast.me_ref, s32[32,1]{1,0:T(8,128)S(1)} %bitcast.5, f32[3,32]{1,0:T(4,128)S(1)} %copy-done.2, bf16[6,64,8192]{2,1,0:T(8,128)(2,1)S(1)} %copy-done), custom_call_target="tpu_custom_call" | custom-call | flops 1179648 | bytes 786432 | tf_op jit(solution)/shard_map/pallas_call | solution.py:264
  26.1 1.6 %collective-permute-start.6 = (s16[1,784,128]{2,1,0:T(8,128)(2,1)S(1)}, s16[1,784,128]{2,1,0:T(8,128)(2,1)S(1)}, u32[]{:S(2)}, u32[]{:S(2)}) collective-permute-start(s16[1,784,128]{2,1,0:T(8,128)(2,1)S(1)} %shard_map.53), channel_id=1, source_target_pairs={{0,4},{4,0},{8,12},{12,8},{16,20},{20,16},{24,28},{28,24},{1,5},{5... | collective-permute-start | bytes 602120 | tf_op jit(solution)/shard_map/ppermute | solution.py:389
  27.7 1.3 %shard_map.46 = (s16[1,784,128]{2,1,0:T(8,128)(2,1)S(1)}, s16[1,784,128]{2,1,0:T(8,128)(2,1)S(1)}) custom-call(s32[1]{0:T(128)} %bitcast.me_ref, s32[32,1]{1,0:T(8,128)S(1)} %bitcast.6, f32[3,32]{1,0:T(4,128)S(1)} %copy-done.2, bf16[6,64,8192]{2,1,0:T(8,128)(2,1)S(1)} %copy-done), custom_call_target="tpu_custom_call" | custom-call | flops 2359296 | bytes 1572864 | tf_op jit(solution)/shard_map/pallas_call | solution.py:264
  29.6 1.1 %shard_map.57 = s16[1,784,128]{2,1,0:T(8,128)(2,1)S(1)} custom-call(s32[1]{0:T(128)} %bitcast.me_ref, s32[32,1]{1,0:T(8,128)S(1)} %bitcast.7, f32[3,32]{1,0:T(4,128)S(1)} %copy-done.2, bf16[6,64,8192]{2,1,0:T(8,128)(2,1)S(1)} %copy-done), custom_call_target="tpu_custom_call" | custom-call | flops 1179648 | bytes 786432 | tf_op jit(solution)/shard_map/pallas_call | solution.py:264
  30.7 1.2 %shard_map.55 = s16[1,784,128]{2,1,0:T(8,128)(2,1)S(1)} custom-call(s32[1]{0:T(128)} %bitcast.me_ref, s32[32,1]{1,0:T(8,128)S(1)} %bitcast.8, f32[3,32]{1,0:T(4,128)S(1)} %copy-done.2, bf16[6,64,8192]{2,1,0:T(8,128)(2,1)S(1)} %copy-done, s16[1,784,128]{2,1,0:T(8,128)(2,1)S(1)} %collective-permute-done.7.refs_0_), custom_call_target="tpu_custom_call" | custom-call | flops 1179648 | bytes 786432 | tf_op jit(solution)/shard_map/pallas_call | solution.py:264
  32.6 1.4 %collective-permute-start.10 = (s16[1,784,128]{2,1,0:T(8,128)(2,1)S(1)}, s16[1,784,128]{2,1,0:T(8,128)(2,1)S(1)}, u32[]{:S(2)}, u32[]{:S(2)}) collective-permute-start(s16[1,784,128]{2,1,0:T(8,128)(2,1)S(1)} %shard_map.57), channel_id=1, source_target_pairs={{0,8},{4,12},{8,0},{12,4},{16,24},{20,28},{24,16},{28,20},{1,9},{5... | collective-permute-start | bytes 602120 | tf_op jit(solution)/shard_map/ppermute | solution.py:389
  34.0 1.2 %shard_map.58 = s16[1,784,128]{2,1,0:T(8,128)(2,1)S(1)} custom-call(s32[1]{0:T(128)} %bitcast.me_ref, s32[32,1]{1,0:T(8,128)S(1)} %bitcast.9, f32[3,32]{1,0:T(4,128)S(1)} %copy-done.2, bf16[6,64,8192]{2,1,0:T(8,128)(2,1)S(1)} %copy-done, s16[1,784,128]{2,1,0:T(8,128)(2,1)S(1)} %collective-permute-done.11.refs_0_), custom_call_target="tpu_custom_call" | custom-call | flops 1179648 | bytes 786432 | tf_op jit(solution)/shard_map/pallas_call | solution.py:264
  35.2 1.6 %collective-permute-start.12 = (s16[1,784,128]{2,1,0:T(8,128)(2,1)S(1)}, s16[1,784,128]{2,1,0:T(8,128)(2,1)S(1)}, u32[]{:S(2)}, u32[]{:S(2)}) collective-permute-start(s16[1,784,128]{2,1,0:T(8,128)(2,1)S(1)} %shard_map.58), channel_id=1, source_target_pairs={{0,4},{4,0},{8,12},{12,8},{16,20},{20,16},{24,28},{28,24},{1,5},{5... | collective-permute-start | bytes 602120 | tf_op jit(solution)/shard_map/ppermute | solution.py:389
  37.3 1.8 %shard_map.48 = bf16[1,6,32,1024]{3,2,1,0:T(8,128)(2,1)} custom-call(s32[1]{0:T(128)} %bitcast.me_ref, bf16[6,64,8192]{2,1,0:T(8,128)(2,1)} %x_ref.27), custom_call_target="tpu_custom_call" | custom-call | flops 393216 | bytes 1572864 | tf_op jit(solution)/shard_map/pallas_call | solution.py:224
  39.1 0.7 %collective-permute-start.1 = (bf16[1,6,32,1024]{3,2,1,0:T(8,128)(2,1)}, bf16[1,6,32,1024]{3,2,1,0:T(8,128)(2,1)S(1)}, u32[]{:S(2)}, u32[]{:S(2)}) collective-permute-start(bf16[1,6,32,1024]{3,2,1,0:T(8,128)(2,1)} %shard_map.48), channel_id=1, source_target_pairs={{0,8},{4,12},{8,0},{12,4},{16,24},{20,28},{24,16},{28,20},{1,9},{5... | collective-permute-start | bytes 1179656 | tf_op jit(solution)/shard_map/ppermute | solution.py:373
  39.7 2.8 %copy-done.1 = bf16[6,64,8192]{2,1,0:T(8,128)(2,1)S(1)} copy-done((bf16[6,64,8192]{2,1,0:T(8,128)(2,1)S(1)}, bf16[6,64,8192]{2,1,0:T(8,128)(2,1)}, u32[]{:S(2)}) %copy-start.1) | copy-done | bytes 6291480
  42.5 1.2 %shard_map.52 = s16[1,784,128]{2,1,0:T(8,128)(2,1)S(1)} custom-call(s32[1]{0:T(128)} %bitcast.me_ref, s32[32,1]{1,0:T(8,128)S(1)} %bitcast.10, f32[3,32]{1,0:T(4,128)S(1)} %copy-done.3, bf16[6,64,8192]{2,1,0:T(8,128)(2,1)S(1)} %copy-done.1, s16[1,784,128]{2,1,0:T(8,128)(2,1)S(1)} %collective-permute-done.4.refs_0_), custom_call_target="tpu_custom_call" | custom-call | flops 1179648 | bytes 786432 | tf_op jit(solution)/shard_map/pallas_call | solution.py:264
  43.7 1.2 %shard_map.50 = s16[1,784,128]{2,1,0:T(8,128)(2,1)S(1)} custom-call(s32[1]{0:T(128)} %bitcast.me_ref, s32[32,1]{1,0:T(8,128)S(1)} %bitcast.11, f32[3,32]{1,0:T(4,128)S(1)} %copy-done.3, bf16[6,64,8192]{2,1,0:T(8,128)(2,1)S(1)} %copy-done.1, s16[1,784,128]{2,1,0:T(8,128)(2,1)S(1)} %collective-permute-done.2.refs_0_), custom_call_target="tpu_custom_call" | custom-call | flops 1179648 | bytes 786432 | tf_op jit(solution)/shard_map/pallas_call | solution.py:264
  44.9 1.6 %collective-permute-start.5 = (s16[1,784,128]{2,1,0:T(8,128)(2,1)S(1)}, s16[1,784,128]{2,1,0:T(8,128)(2,1)S(1)}, u32[]{:S(2)}, u32[]{:S(2)}) collective-permute-start(s16[1,784,128]{2,1,0:T(8,128)(2,1)S(1)} %shard_map.52), channel_id=1, source_target_pairs={{0,4},{4,0},{8,12},{12,8},{16,20},{20,16},{24,28},{28,24},{1,5},{5... | collective-permute-start | bytes 602120 | tf_op jit(solution)/shard_map/ppermute | solution.py:389
  46.4 1.2 %shard_map.56 = s16[1,784,128]{2,1,0:T(8,128)(2,1)S(1)} custom-call(s32[1]{0:T(128)} %bitcast.me_ref, s32[32,1]{1,0:T(8,128)S(1)} %bitcast.12, f32[3,32]{1,0:T(4,128)S(1)} %copy-done.3, bf16[6,64,8192]{2,1,0:T(8,128)(2,1)S(1)} %copy-done.1, s16[1,784,128]{2,1,0:T(8,128)(2,1)S(1)} %collective-permute-done.6.refs_0_, ...), custom_call_target="tpu_custom_call" | custom-call | flops 1179648 | bytes 786432 | tf_op jit(solution)/shard_map/pallas_call | solution.py:264
  47.6 1.5 %collective-permute-start.3 = (s16[1,784,128]{2,1,0:T(8,128)(2,1)S(1)}, s16[1,784,128]{2,1,0:T(8,128)(2,1)S(1)}, u32[]{:S(2)}, u32[]{:S(2)}) collective-permute-start(s16[1,784,128]{2,1,0:T(8,128)(2,1)S(1)} %shard_map.50), channel_id=1, source_target_pairs={{0,8},{4,12},{8,0},{12,4},{16,24},{20,28},{24,16},{28,20},{1,9},{5... | collective-permute-start | bytes 602120 | tf_op jit(solution)/shard_map/ppermute | solution.py:389
  49.1 0.8 %collective-permute-start.9 = (s16[1,784,128]{2,1,0:T(8,128)(2,1)S(1)}, s16[1,784,128]{2,1,0:T(8,128)(2,1)S(1)}, u32[]{:S(2)}, u32[]{:S(2)}) collective-permute-start(s16[1,784,128]{2,1,0:T(8,128)(2,1)S(1)} %shard_map.56), channel_id=1, source_target_pairs={{0,16},{4,20},{8,24},{12,28},{16,0},{20,4},{24,8},{28,12},{1,17},{... | collective-permute-start | bytes 602120 | tf_op jit(solution)/shard_map/ppermute | solution.py:389
  49.9 1.2 %shard_map.59 = s16[1,784,128]{2,1,0:T(8,128)(2,1)S(1)} custom-call(s32[1]{0:T(128)} %bitcast.me_ref, s32[32,1]{1,0:T(8,128)S(1)} %bitcast.13, f32[3,32]{1,0:T(4,128)S(1)} %copy-done.3, bf16[6,64,8192]{2,1,0:T(8,128)(2,1)S(1)} %copy-done.1, s16[1,784,128]{2,1,0:T(8,128)(2,1)S(1)} %collective-permute-done.10.refs_0_, ...), custom_call_target="tpu_custom_call" | custom-call | flops 1179648 | bytes 786432 | tf_op jit(solution)/shard_map/pallas_call | solution.py:264
  51.1 2.2 %collective-permute-start.13 = (s16[1,784,128]{2,1,0:T(8,128)(2,1)S(1)}, s16[1,784,128]{2,1,0:T(8,128)(2,1)S(1)}, u32[]{:S(2)}, u32[]{:S(2)}) collective-permute-start(s16[1,784,128]{2,1,0:T(8,128)(2,1)S(1)} %shard_map.59), channel_id=1, source_target_pairs={{0,16},{4,20},{8,24},{12,28},{16,0},{20,4},{24,8},{28,12},{1,17},{... | collective-permute-start | bytes 602120 | tf_op jit(solution)/shard_map/ppermute | solution.py:389
  53.4 1.1 %shard_map.47.refs_0_ = f32[3,32,1024]{2,1,0:T(8,128)S(1)} custom-call(s32[1]{0:T(128)} %bitcast.me_ref, s32[32,1]{1,0:T(8,128)S(1)} %bitcast.14, f32[3,32]{1,0:T(4,128)S(1)} %copy-done.3, bf16[6,64,8192]{2,1,0:T(8,128)(2,1)S(1)} %copy-done.1, s16[1,784,128]{2,1,0:T(8,128)(2,1)S(1)} %collective-permute-done.piece_ref), custom_call_target="tpu_custom_call" | custom-call | flops 1179648 | bytes 786432 | tf_op jit(solution)/shard_map/pallas_call | solution.py:285
  54.4 3.2 %collective-permute-done.1.piece_ref = bf16[1,6,32,1024]{3,2,1,0:T(8,128)(2,1)S(1)} collective-permute-done((bf16[1,6,32,1024]{3,2,1,0:T(8,128)(2,1)}, bf16[1,6,32,1024]{3,2,1,0:T(8,128)(2,1)S(1)}, u32[]{:S(2)}, u32[]{:S(2)}) %collective-permute-start.1) | collective-permute-done | bytes 393248 | tf_op jit(solution)/shard_map/ppermute | solution.py:373
  57.6 1.3 %shard_map.49.refs_1_ = f32[3,32,1024]{2,1,0:T(8,128)S(1)} custom-call(s32[1]{0:T(128)} %bitcast.me_ref, s32[32,1]{1,0:T(8,128)S(1)} %bitcast.15, f32[3,32]{1,0:T(4,128)S(1)} %copy-done.3, bf16[6,64,8192]{2,1,0:T(8,128)(2,1)S(1)} %copy-done.1, bf16[1,6,32,1024]{3,2,1,0:T(8,128)(2,1)S(1)} %collective-permute-done.1.piece_ref), custom_call_target="tpu_custom_call" | custom-call | flops 1179648 | bytes 786432 | tf_op jit(solution)/shard_map/pallas_call | solution.py:285
  58.9 0.8 %collective-permute-done.3.refs_2_ = s16[1,784,128]{2,1,0:T(8,128)(2,1)S(1)} collective-permute-done((s16[1,784,128]{2,1,0:T(8,128)(2,1)S(1)}, s16[1,784,128]{2,1,0:T(8,128)(2,1)S(1)}, u32[]{:S(2)}, u32[]{:S(2)}) %collective-permute-start.3) | collective-permute-done | bytes 200736 | tf_op jit(solution)/shard_map/ppermute | solution.py:389
  59.7 4.5 %collective-permute-done.9.refs_4_ = s16[1,784,128]{2,1,0:T(8,128)(2,1)S(1)} collective-permute-done((s16[1,784,128]{2,1,0:T(8,128)(2,1)S(1)}, s16[1,784,128]{2,1,0:T(8,128)(2,1)S(1)}, u32[]{:S(2)}, u32[]{:S(2)}) %collective-permute-start.9) | collective-permute-done | bytes 200736 | tf_op jit(solution)/shard_map/ppermute | solution.py:389
  64.2 2.1 %collective-permute-done.13.refs_5_ = s16[1,784,128]{2,1,0:T(8,128)(2,1)S(1)} collective-permute-done((s16[1,784,128]{2,1,0:T(8,128)(2,1)S(1)}, s16[1,784,128]{2,1,0:T(8,128)(2,1)S(1)}, u32[]{:S(2)}, u32[]{:S(2)}) %collective-permute-start.13) | collective-permute-done | bytes 200736 | tf_op jit(solution)/shard_map/ppermute | solution.py:389
  66.4 1.0 %shard_map.60 = bf16[3,64,1024]{2,1,0:T(8,128)(2,1)} custom-call(f32[3,32,1024]{2,1,0:T(8,128)S(1)} %shard_map.47.refs_0_, f32[3,32,1024]{2,1,0:T(8,128)S(1)} %shard_map.49.refs_1_, s16[1,784,128]{2,1,0:T(8,128)(2,1)S(1)} %collective-permute-done.3.refs_2_, s16[1,784,128]{2,1,0:T(8,128)(2,1)S(1)} %collective-permute-done.5.refs_3_, ...), custom_call_target="tpu_custom_call" | custom-call | flops 786432 | bytes 1572864 | tf_op jit(solution)/shard_map/pallas_call | solution.py:304
  (22 shorter events, 4.4 us)
Async XLA Ops:
  1.9 14.4 %all-to-all-start = ((s32[32,1,1]{2,1,0:T(1,128)}), s32[32,1,1]{2,1,0:T(1,128)S(1)}, u32[]{:S(2)}, u32[]{:S(2)}) async-start(s32[32,1,1]{2,1,0:T(1,128)} %broadcast_in_dim.9), calls=%async_computation | async-start | bytes 32768 | tf_op jit(solution)/shard_map/all_to_all | solution.py:362
  16.3 2.8 %copy-start = (bf16[6,64,8192]{2,1,0:T(8,128)(2,1)S(1)}, bf16[6,64,8192]{2,1,0:T(8,128)(2,1)}, u32[]{:S(2)}) copy-start(bf16[6,64,8192]{2,1,0:T(8,128)(2,1)} %x_ref.27) | copy-start | bytes 18874372
  19.1 0.7 %copy-start.2 = (f32[3,32]{1,0:T(4,128)S(1)}, f32[3,32]{1,0:T(4,128)}, u32[]{:S(2)}) copy-start(f32[3,32]{1,0:T(4,128)} %coef_ref.25) | copy-start | bytes 1156
  21.2 9.6 %collective-permute-start.7 = (s16[1,784,128]{2,1,0:T(8,128)(2,1)S(1)}, s16[1,784,128]{2,1,0:T(8,128)(2,1)S(1)}, u32[]{:S(2)}, u32[]{:S(2)}) collective-permute-start(s16[1,784,128]{2,1,0:T(8,128)(2,1)S(1)} %get-tuple-element.11), channel_id=1, source_target_pairs={{0,4},{4,0},{8,12},{12,8},{16,20},{20,16},{24,28},{28,24},{1,5},{5... | collective-permute-start | bytes 602120 | tf_op jit(solution)/shard_map/ppermute | solution.py:389
  21.8 10.8 %collective-permute-start.11 = (s16[1,784,128]{2,1,0:T(8,128)(2,1)S(1)}, s16[1,784,128]{2,1,0:T(8,128)(2,1)S(1)}, u32[]{:S(2)}, u32[]{:S(2)}) collective-permute-start(s16[1,784,128]{2,1,0:T(8,128)(2,1)S(1)} %get-tuple-element.12), channel_id=1, source_target_pairs={{0,8},{4,12},{8,0},{12,4},{16,24},{20,28},{24,16},{28,20},{1,9},{5... | collective-permute-start | bytes 602120 | tf_op jit(solution)/shard_map/ppermute | solution.py:389
  23.5 11.7 %collective-permute-start.4 = (s16[1,784,128]{2,1,0:T(8,128)(2,1)S(1)}, s16[1,784,128]{2,1,0:T(8,128)(2,1)S(1)}, u32[]{:S(2)}, u32[]{:S(2)}) collective-permute-start(s16[1,784,128]{2,1,0:T(8,128)(2,1)S(1)} %shard_map.51), channel_id=1, source_target_pairs={{0,8},{4,12},{8,0},{12,4},{16,24},{20,28},{24,16},{28,20},{1,9},{5... | collective-permute-start | bytes 602120 | tf_op jit(solution)/shard_map/ppermute | solution.py:389
  26.1 10.6 %collective-permute-start.6 = (s16[1,784,128]{2,1,0:T(8,128)(2,1)S(1)}, s16[1,784,128]{2,1,0:T(8,128)(2,1)S(1)}, u32[]{:S(2)}, u32[]{:S(2)}) collective-permute-start(s16[1,784,128]{2,1,0:T(8,128)(2,1)S(1)} %shard_map.53), channel_id=1, source_target_pairs={{0,4},{4,0},{8,12},{12,8},{16,20},{20,16},{24,28},{28,24},{1,5},{5... | collective-permute-start | bytes 602120 | tf_op jit(solution)/shard_map/ppermute | solution.py:389
  29.0 10.0 %collective-permute-start.2 = (s16[1,784,128]{2,1,0:T(8,128)(2,1)S(1)}, s16[1,784,128]{2,1,0:T(8,128)(2,1)S(1)}, u32[]{:S(2)}, u32[]{:S(2)}) collective-permute-start(s16[1,784,128]{2,1,0:T(8,128)(2,1)S(1)} %get-tuple-element.10), channel_id=1, source_target_pairs={{0,4},{4,0},{8,12},{12,8},{16,20},{20,16},{24,28},{28,24},{1,5},{5... | collective-permute-start | bytes 602120 | tf_op jit(solution)/shard_map/ppermute | solution.py:389
  31.9 7.8 %copy-start.3 = (f32[3,32]{1,0:T(4,128)S(1)}, f32[3,32]{1,0:T(4,128)}, u32[]{:S(2)}) copy-start(f32[3,32]{1,0:T(4,128)} %coef_ref.25) | copy-start | bytes 1156
  31.9 12.9 %collective-permute-start.8 = (s16[1,784,128]{2,1,0:T(8,128)(2,1)S(1)}, s16[1,784,128]{2,1,0:T(8,128)(2,1)S(1)}, u32[]{:S(2)}, u32[]{:S(2)}) collective-permute-start(s16[1,784,128]{2,1,0:T(8,128)(2,1)S(1)} %shard_map.55), channel_id=1, source_target_pairs={{0,8},{4,12},{8,0},{12,4},{16,24},{20,28},{24,16},{28,20},{1,9},{5... | collective-permute-start | bytes 602120 | tf_op jit(solution)/shard_map/ppermute | solution.py:389
  32.6 15.0 %collective-permute-start.10 = (s16[1,784,128]{2,1,0:T(8,128)(2,1)S(1)}, s16[1,784,128]{2,1,0:T(8,128)(2,1)S(1)}, u32[]{:S(2)}, u32[]{:S(2)}) collective-permute-start(s16[1,784,128]{2,1,0:T(8,128)(2,1)S(1)} %shard_map.57), channel_id=1, source_target_pairs={{0,8},{4,12},{8,0},{12,4},{16,24},{20,28},{24,16},{28,20},{1,9},{5... | collective-permute-start | bytes 602120 | tf_op jit(solution)/shard_map/ppermute | solution.py:389
  35.2 13.9 %collective-permute-start.12 = (s16[1,784,128]{2,1,0:T(8,128)(2,1)S(1)}, s16[1,784,128]{2,1,0:T(8,128)(2,1)S(1)}, u32[]{:S(2)}, u32[]{:S(2)}) collective-permute-start(s16[1,784,128]{2,1,0:T(8,128)(2,1)S(1)} %shard_map.58), channel_id=1, source_target_pairs={{0,4},{4,0},{8,12},{12,8},{16,20},{20,16},{24,28},{28,24},{1,5},{5... | collective-permute-start | bytes 602120 | tf_op jit(solution)/shard_map/ppermute | solution.py:389
  36.7 14.4 %collective-permute-start = (s16[1,784,128]{2,1,0:T(8,128)(2,1)S(1)}, s16[1,784,128]{2,1,0:T(8,128)(2,1)S(1)}, u32[]{:S(2)}, u32[]{:S(2)}) collective-permute-start(s16[1,784,128]{2,1,0:T(8,128)(2,1)S(1)} %get-tuple-element.9), channel_id=1, source_target_pairs={{0,4},{4,0},{8,12},{12,8},{16,20},{20,16},{24,28},{28,24},{1,5},{5... | collective-permute-start | bytes 602120 | tf_op jit(solution)/shard_map/ppermute | solution.py:389
  39.1 18.5 %collective-permute-start.1 = (bf16[1,6,32,1024]{3,2,1,0:T(8,128)(2,1)}, bf16[1,6,32,1024]{3,2,1,0:T(8,128)(2,1)S(1)}, u32[]{:S(2)}, u32[]{:S(2)}) collective-permute-start(bf16[1,6,32,1024]{3,2,1,0:T(8,128)(2,1)} %shard_map.48), channel_id=1, source_target_pairs={{0,8},{4,12},{8,0},{12,4},{16,24},{20,28},{24,16},{28,20},{1,9},{5... | collective-permute-start | bytes 1179656 | tf_op jit(solution)/shard_map/ppermute | solution.py:373
  39.7 2.8 %copy-start.1 = (bf16[6,64,8192]{2,1,0:T(8,128)(2,1)S(1)}, bf16[6,64,8192]{2,1,0:T(8,128)(2,1)}, u32[]{:S(2)}) copy-start(bf16[6,64,8192]{2,1,0:T(8,128)(2,1)} %x_ref.27) | copy-start | bytes 18874372
  44.9 14.0 %collective-permute-start.5 = (s16[1,784,128]{2,1,0:T(8,128)(2,1)S(1)}, s16[1,784,128]{2,1,0:T(8,128)(2,1)S(1)}, u32[]{:S(2)}, u32[]{:S(2)}) collective-permute-start(s16[1,784,128]{2,1,0:T(8,128)(2,1)S(1)} %shard_map.52), channel_id=1, source_target_pairs={{0,4},{4,0},{8,12},{12,8},{16,20},{20,16},{24,28},{28,24},{1,5},{5... | collective-permute-start | bytes 602120 | tf_op jit(solution)/shard_map/ppermute | solution.py:389
  47.6 12.1 %collective-permute-start.3 = (s16[1,784,128]{2,1,0:T(8,128)(2,1)S(1)}, s16[1,784,128]{2,1,0:T(8,128)(2,1)S(1)}, u32[]{:S(2)}, u32[]{:S(2)}) collective-permute-start(s16[1,784,128]{2,1,0:T(8,128)(2,1)S(1)} %shard_map.50), channel_id=1, source_target_pairs={{0,8},{4,12},{8,0},{12,4},{16,24},{20,28},{24,16},{28,20},{1,9},{5... | collective-permute-start | bytes 602120 | tf_op jit(solution)/shard_map/ppermute | solution.py:389
  49.1 15.1 %collective-permute-start.9 = (s16[1,784,128]{2,1,0:T(8,128)(2,1)S(1)}, s16[1,784,128]{2,1,0:T(8,128)(2,1)S(1)}, u32[]{:S(2)}, u32[]{:S(2)}) collective-permute-start(s16[1,784,128]{2,1,0:T(8,128)(2,1)S(1)} %shard_map.56), channel_id=1, source_target_pairs={{0,16},{4,20},{8,24},{12,28},{16,0},{20,4},{24,8},{28,12},{1,17},{... | collective-permute-start | bytes 602120 | tf_op jit(solution)/shard_map/ppermute | solution.py:389
  51.1 15.2 %collective-permute-start.13 = (s16[1,784,128]{2,1,0:T(8,128)(2,1)S(1)}, s16[1,784,128]{2,1,0:T(8,128)(2,1)S(1)}, u32[]{:S(2)}, u32[]{:S(2)}) collective-permute-start(s16[1,784,128]{2,1,0:T(8,128)(2,1)S(1)} %shard_map.59), channel_id=1, source_target_pairs={{0,16},{4,20},{8,24},{12,28},{16,0},{20,4},{24,8},{28,12},{1,17},{... | collective-permute-start | bytes 602120 | tf_op jit(solution)/shard_map/ppermute | solution.py:389
